TPU v7x, 32 devices: a whole 2x2x4 slice. The times are simulated.
32 devices in a mesh: chan: 4 (over z), pulse: 4 (over x, core), range: 2 (over y).
Axes of the slice: x: 2, y: 2, z: 4, core: 2. Of those that a mesh axis runs over, the one named last changes fastest.
Arguments:
- signal: bfloat16 [2, 64, 32, 8192], P(None, 'chan', 'pulse', 'range'), may hold values from -6 to 6
- steering: bfloat16 [2, 32, 64], replicated, may hold values from -0.5 to 0.5
- spectrum: float32 [2, 8192], replicated, may hold values from -6 to 6
Outputs:
- detection: float32 [32, 32, 8192], P('chan', 'pulse', 'range')
All inputs are finite; a program needn't handle non-finite values.
Results may differ from a plain program's by a relative error of at most 0.0087.
Values may be sent and summed in bfloat16 or wider, within the bound.
A program may use at most 64 MiB of HBM per device.

v0:
```python
import math
import jax
import jax.numpy as jnp
from jax import lax
from jax.sharding import PartitionSpec as P

GUARD = 4
TRAIN = 16
PRECISE = lax.Precision.HIGHEST
NOISE_FLOOR = 0.25


def padded_2(x, sides, width):
    for axis, dim in sides:
        peers, length = (lax.axis_size(axis), x.shape[dim])
        up = [(i, (i + 1) % peers) for i in range(peers - 1)]
        down = [(j, i) for i, j in up]
        last = lax.slice_in_dim(x, length - width, length, axis=dim)
        initial = lax.slice_in_dim(x, 0, width, axis=dim)
        before = lax.ppermute(last, axis, up)
        after = lax.ppermute(initial, axis, down)
        x = jnp.concatenate([before, x, after], axis=dim)
    return x


def doppler_tables(pulse_count):
    row_ids = lax.broadcasted_iota(jnp.int32, (pulse_count, pulse_count), 0)
    col_ids = lax.broadcasted_iota(jnp.int32, (pulse_count, pulse_count), 1)
    phase_angle = (row_ids * col_ids % pulse_count).astype(jnp.float32) * (
        2.0 * math.pi / pulse_count
    )
    norm_scale = 1.0 / math.sqrt(pulse_count)
    table_real = (jnp.cos(phase_angle) * norm_scale).astype(jnp.bfloat16)
    table_imag = (-jnp.sin(phase_angle) * norm_scale).astype(jnp.bfloat16)
    return (table_real, table_imag)


def phase_table(row_count, col_count, period_len, direction):
    row_ids = lax.broadcasted_iota(jnp.int32, (row_count, col_count), 0)
    col_ids = lax.broadcasted_iota(jnp.int32, (row_count, col_count), 1)
    phase_angle = (row_ids * col_ids % period_len).astype(jnp.float32) * (
        2.0 * math.pi / period_len
    )
    return (jnp.cos(phase_angle), direction * jnp.sin(phase_angle))


def rotate_by(field_pair, table_pair):
    return (
        field_pair[0] * table_pair[0] - field_pair[1] * table_pair[1],
        field_pair[0] * table_pair[1] + field_pair[1] * table_pair[0],
    )


def mix_blocks(table_pair, field_pair):

    def contract(table_part, field_part):
        return jnp.einsum("km,bpmn->bpkn", table_part, field_part, precision=PRECISE)

    return (
        contract(table_pair[0], field_pair[0]) - contract(table_pair[1], field_pair[1]),
        contract(table_pair[0], field_pair[1]) + contract(table_pair[1], field_pair[0]),
    )


def mix_lanes(field_pair, table_pair):

    def contract(field_part, table_part):
        return jnp.einsum("bpkm,mn->bpkn", field_part, table_part, precision=PRECISE)

    return (
        contract(field_pair[0], table_pair[0]) - contract(field_pair[1], table_pair[1]),
        contract(field_pair[0], table_pair[1]) + contract(field_pair[1], table_pair[0]),
    )


def local_transform(field_pair, direction):
    size_all = field_pair[0].shape[-1]
    blocks = size_all // 128
    leading = field_pair[0].shape[:-1]
    shaped = tuple((member.reshape(leading + (blocks, 128)) for member in field_pair))
    outer_table = phase_table(blocks, blocks, blocks, direction)
    twiddle = phase_table(blocks, 128, size_all, direction)
    inner_table = phase_table(128, 128, 128, direction)
    if direction < 0:
        shaped = mix_blocks(outer_table, shaped)
        shaped = rotate_by(shaped, twiddle)
        shaped = mix_lanes(shaped, inner_table)
    else:
        shaped = mix_lanes(shaped, inner_table)
        shaped = rotate_by(shaped, twiddle)
        shaped = mix_blocks(outer_table, shaped)
    return tuple((member.reshape(leading + (size_all,)) for member in shaped))


def stack_weights(w_real, w_imag):
    return jnp.concatenate(
        [jnp.concatenate([w_real, -w_imag], 1), jnp.concatenate([w_imag, w_real], 1)], 0
    )


def shards(signal, steering, spectrum):
    beam_count = steering.shape[1]
    chan_count = steering.shape[2]
    pulse_local = signal.shape[2]
    gate_count = signal.shape[3]
    stacked = stack_weights(steering[0], steering[1])
    samples = lax.all_to_all(signal, "chan", split_axis=2, concat_axis=1, tiled=True)
    pulses_here = samples.shape[2]
    gates_here = samples.shape[3]
    flat_samples = samples.reshape(2 * chan_count, pulses_here * gates_here)
    formed = jnp.dot(stacked, flat_samples, preferred_element_type=jnp.float32)
    formed = formed.astype(jnp.bfloat16).reshape(2, beam_count, pulses_here, gates_here)
    beam_data = lax.all_to_all(formed, "chan", split_axis=1, concat_axis=2, tiled=True)
    beam_local = beam_data.shape[1]
    range_count = lax.axis_size("range")
    range_index = lax.axis_index("range")
    full_length = gate_count * range_count
    inverse_scale = 1.0 / full_length
    shard_piece = lax.all_gather(beam_data, "range", axis=3, tiled=True)
    shard_count = shard_piece.shape[3] // gate_count
    members = shard_piece.astype(jnp.float32).reshape(
        2, beam_local, pulse_local, shard_count, gate_count
    )
    source = jnp.arange(shard_count, dtype=jnp.int32)
    phase_angle = (source * range_index % range_count).astype(jnp.float32) * (
        2.0 * math.pi / range_count
    )
    cos_part = jnp.cos(phase_angle)[:, None]
    sin_part = -jnp.sin(phase_angle)[:, None]
    sum_real = jnp.sum(members[0] * cos_part - members[1] * sin_part, axis=2)
    sum_imag = jnp.sum(members[0] * sin_part + members[1] * cos_part, axis=2)
    folded = (sum_real, sum_imag)
    gate_ids = lax.broadcasted_iota(jnp.int32, (gate_count,), 0)
    global_angle = (gate_ids * range_index % full_length).astype(jnp.float32) * (
        2.0 * math.pi / full_length
    )
    folded = rotate_by(folded, (jnp.cos(global_angle), -jnp.sin(global_angle)))
    spectrum_local = local_transform(folded, -1.0)
    response = spectrum.reshape(2, gate_count, range_count)
    response = lax.dynamic_index_in_dim(response, range_index, axis=2, keepdims=False)
    response = jnp.transpose(response.reshape(2, 128, gate_count // 128), (0, 2, 1)).reshape(
        2, gate_count
    )
    filtered = rotate_by(spectrum_local, (response[0], response[1]))
    restored = local_transform(filtered, 1.0)
    restored = rotate_by(restored, (jnp.cos(global_angle), jnp.sin(global_angle)))
    shard_piece = (
        lax.all_gather(restored[0], "range", axis=2, tiled=True),
        lax.all_gather(restored[1], "range", axis=2, tiled=True),
    )
    shard_count = shard_piece[0].shape[2] // gate_count
    rows_real = shard_piece[0].reshape(beam_local, pulse_local, shard_count, gate_count)
    rows_imag = shard_piece[1].reshape(beam_local, pulse_local, shard_count, gate_count)
    source = jnp.arange(shard_count, dtype=jnp.int32)
    phase_angle = (source * range_index % range_count).astype(jnp.float32) * (
        2.0 * math.pi / range_count
    )
    cos_part = jnp.cos(phase_angle)[:, None]
    sin_part = jnp.sin(phase_angle)[:, None]
    sum_real = jnp.sum(rows_real * cos_part - rows_imag * sin_part, axis=2)
    sum_imag = jnp.sum(rows_real * sin_part + rows_imag * cos_part, axis=2)
    compressed = jnp.stack([sum_real * inverse_scale, sum_imag * inverse_scale]).astype(
        jnp.bfloat16
    )
    pulse_total = pulse_local * lax.axis_size("pulse")
    dop_real, dop_imag = doppler_tables(pulse_total)
    columns = lax.all_to_all(compressed, "pulse", split_axis=3, concat_axis=2, tiled=True)

    def product(table_part, values):
        return jnp.einsum("fp,bpr->bfr", table_part, values, preferred_element_type=jnp.float32)

    mixed_real = product(dop_real, columns[0]) - product(dop_imag, columns[1])
    mixed_imag = product(dop_real, columns[1]) + product(dop_imag, columns[0])
    power_part = lax.all_to_all(
        mixed_real * mixed_real + mixed_imag * mixed_imag,
        "pulse",
        split_axis=1,
        concat_axis=2,
        tiled=True,
    )
    halo_width = GUARD + TRAIN
    padded = padded_2(power_part, (("range", 2),), halo_width)
    window_sum = jnp.zeros_like(power_part)
    for offset in range(1, TRAIN + 1):
        left_start = halo_width - GUARD - offset
        right_start = halo_width + GUARD + offset
        window_sum = (
            window_sum
            + padded[:, :, left_start : left_start + gate_count]
            + padded[:, :, right_start : right_start + gate_count]
        )
    noise_level = window_sum / (2.0 * TRAIN)
    return power_part / (noise_level + NOISE_FLOOR)


def solution(mesh):
    in_specs = (P(None, "chan", "pulse", "range"), P(), P())
    out_specs = P("chan", "pulse", "range")
    return jax.shard_map(shards, mesh=mesh, in_specs=in_specs, out_specs=out_specs, check_vma=False)
```

profile of v0, /device:TPU:0, one launch (start us, length us, event | category | flops | bytes accessed | tf_op | source)
XLA Modules:
  0.0 388.4 jit_solution(4963313028370823325)
XLA Ops:
  6.5 4.1 %copy.81 = bf16[2,16,8,4096]{3,1,0,2:T(8,128)(2,1)} copy(bf16[2,16,8,4096]{3,2,1,0:T(8,128)(2,1)} %param.3) | data formatting | bytes 4194304 | tf_op args[0]
  10.6 6.5 %all-to-all-start = ((bf16[2,16,8,4096]{3,1,0,2:T(8,128)(2,1)}), bf16[2,16,8,4096]{3,1,0,2:T(8,128)(2,1)S(1)}, u32[]{:S(2)}, u32[]{:S(2)}) async-start(bf16[2,16,8,4096]{3,1,0,2:T(8,128)(2,1)} %copy.81), calls=%async_computation | async-start | bytes 4194304 | tf_op jit(solution)/shard_map/all_to_all | solution.py:107
  17.1 48.2 %all-to-all-done = bf16[2,16,8,4096]{3,1,0,2:T(8,128)(2,1)S(1)} async-done(((bf16[2,16,8,4096]{3,1,0,2:T(8,128)(2,1)}), bf16[2,16,8,4096]{3,1,0,2:T(8,128)(2,1)S(1)}, u32[]{:S(2)}, u32[]{:S(2)}) %all-to-all-start) | async-done | bytes 2097184 | tf_op jit(solution)/shard_map/all_to_all | solution.py:107
  65.3 2.2 copy.82
  67.5 1.3 copy.126
  68.8 0.5 convolution_convert_fusion
  69.3 0.8 reshape.187
  70.1 0.9 copy.83
  71.0 27.7 %all_to_all.66 = bf16[2,32,2,4096]{3,2,0,1:T(2,128)(2,1)S(1)} all-to-all(bf16[2,32,2,4096]{3,2,0,1:T(2,128)(2,1)S(1)} %copy.83), channel_id=1, replica_groups=mesh['chan'=4,'pulse'=4,'range'=2] {'chan'}, dimensions={1} | all-to-all | bytes 2097152 | tf_op jit(solution)/shard_map/all_to_all | solution.py:113
  98.7 0.6 copy.158
  99.3 1.0 copy.85
  100.4 0.3 all-gather.6.cloned.1.call-start
  100.6 6.4 %reshape.188 = f32[2,4096,2]{2,1,0:T(8,128)} reshape(f32[2,8192]{1,0:T(2,128)S(1)} %copy-done.1) | data formatting | bytes 131072 | tf_op jit(solution)/shard_map/reshape | solution.py:139
  107.0 4.7 %dynamic-slice_reduce_fusion = f32[2,4096]{1,0:T(2,128)S(1)} fusion(f32[2,4096,2]{2,1,0:T(8,128)} %reshape.188, s32[]{:T(128)S(6)} %select_n.134), kind=kLoop, calls=%fused_computation.31 | loop fusion | bytes 65540 | tf_op jit(solution)/shard_map/jit(dynamic_index_in_dim)/dynamic_slice | solution.py:140
  111.8 0.1 reshape.189
  112.5 20.2 %all-gather.4.cloned.1.call-done = bf16[2,8,8,8192]{3,1,2,0:T(8,128)(2,1)} async-done(((bf16[2,8,8,4096]{3,1,2,0:T(8,128)(2,1)}), bf16[2,8,8,8192]{3,1,2,0:T(8,128)(2,1)}) %all-gather.4.cloned.1.call-update) | async-done | bytes 2097168 | tf_op jit(solution)/shard_map/all_gather | solution.py:119
  132.7 3.9 %fusion.271 = (f32[1,8,8,8192]{3,1,2,0:T(8,128)}, f32[1,8,8,8192]{3,1,2,0:T(8,128)}) fusion(bf16[2,8,8,8192]{3,1,2,0:T(8,128)(2,1)} %all-gather.4.cloned.1.call-done), kind=kLoop, calls=%fused_computation.365 | loop fusion | bytes 8388608 | tf_op jit(solution)/shard_map/slice | solution.py:130
  136.6 3.0 reshape.202
  139.7 4.4 %reshape.203 = f32[8,8,2,4096]{3,2,0,1:T(2,128)} reshape(f32[1,8,8,8192]{3,1,2,0:T(8,128)} %get-tuple-element.12) | data formatting | bytes 4194304 | tf_op jit(solution)/shard_map/squeeze | solution.py:130
  144.1 5.8 %subtract_reduce_fusion.1 = (f32[8,8,4096]{2,1,0:T(8,128)S(1)}, f32[8,8,4096]{2,1,0:T(8,128)S(1)}) fusion(f32[8,8,2,4096]{3,2,0,1:T(2,128)} %reshape.203, f32[8,8,2,4096]{3,2,0,1:T(2,128)S(1)} %reshape.202, f32[2]{0:T(128)S(1)} %get-tuple-element.24, f32[2]{0:T(128)S(1)} %get-tuple-element.23), kind=kLoop, calls=%fused_computation.35 | loop fusion | flops 3670016 | bytes 6291472 | tf_op jit(solution)/shard_map/reduce_sum | solution.py:130
  149.8 0.6 copy.157
  150.5 0.6 copy.156
  151.1 1.5 fusion.85
  152.6 1.5 fusion.84
  154.1 1.5 fusion.2
  155.6 1.5 fusion.3
  157.1 1.4 fusion.78
  158.5 1.2 fusion.79
  159.8 1.2 convolution_add_fusion.2
  161.0 1.2 convolution_subtract_fusion.2
  162.2 1.2 fusion.80
  163.5 1.2 fusion.81
  164.7 1.2 convolution_add_fusion.1
  165.9 1.2 convolution_subtract_fusion.1
  167.2 1.2 fusion.83
  168.4 1.4 fusion.82
  169.8 2.2 fusion
  172.0 2.4 reshape.191
  174.3 2.2 fusion.1
  176.5 1.5 reshape.190
  178.1 1.6 multiply_subtract_fusion
  179.7 0.7 all-gather.8.cloned.1.call-update
  180.4 32.5 %all-gather.6.cloned.1.call-done = f32[8,8,8192]{2,1,0:T(8,128)} async-done(((f32[8,8,4096]{2,1,0:T(8,128)}), f32[8,8,8192]{2,1,0:T(8,128)}) %all-gather.6.cloned.1.call-update) | async-done | bytes 2097168 | tf_op jit(solution)/shard_map/all_gather | solution.py:148
  212.9 34.7 %all-gather.8.cloned.1.call-done = f32[8,8,8192]{2,1,0:T(8,128)} async-done(((f32[8,8,4096]{2,1,0:T(8,128)}), f32[8,8,8192]{2,1,0:T(8,128)}) %all-gather.8.cloned.1.call-update) | async-done | bytes 2097168 | tf_op jit(solution)/shard_map/all_gather | solution.py:149
  247.6 3.2 subtract_reduce_fusion
  250.7 0.6 fusion.74
  251.3 0.6 fusion.75
  252.1 14.0 %copy.106 = bf16[2,8,8,4096]{2,1,0,3:T(8,128)(2,1)} copy(bf16[2,8,8,4096]{3,1,2,0:T(8,128)(2,1)S(1)} %pad_maximum_fusion.2) | data formatting | bytes 2097152 | tf_op jit(solution)/shard_map/stack | solution.py:162
  266.1 20.5 %reshape.205 = bf16[4,2,65536]{2,1,0:T(2,128)(2,1)S(1)} reshape(bf16[4096,2,8,8]{3,2,1,0:T(8,128)(2,1)} %bitcast.133) | data formatting | bytes 2097152
  286.6 17.2 %all_to_all.67 = bf16[4,2,65536]{2,1,0:T(2,128)(2,1)S(1)} all-to-all(bf16[4,2,65536]{2,1,0:T(2,128)(2,1)S(1)} %reshape.205), channel_id=1, replica_groups=mesh['chan'=4,'pulse'=4,'range'=2] {'pulse'}, dimensions={0} | all-to-all | bytes 2097152 | tf_op jit(solution)/shard_map/all_to_all | solution.py:167
  303.8 21.7 %reshape.206 = bf16[4096,2,8,8]{3,2,1,0:T(8,128)(2,1)} reshape(bf16[4,2,65536]{2,1,0:T(2,128)(2,1)S(1)} %all_to_all.67) | data formatting | bytes 2097152
  325.5 16.0 %copy.107 = bf16[2,8,8,4,1024]{4,2,3,1,0:T(8,128)(2,1)S(1)} copy(bf16[2,8,8,4,1024]{2,1,0,4,3:T(8,128)(2,1)} %bitcast.134) | data formatting | bytes 2097152 | tf_op jit(solution)/shard_map/all_to_all | solution.py:167
  341.5 0.4 fusion.76
  341.9 0.4 fusion.77
  342.3 0.4 fusion.7
  342.7 0.4 fusion.6
  343.0 0.6 copy.108
  343.6 16.9 %all_to_all.68 = f32[8,32,1024]{2,0,1:T(8,128)S(1)} all-to-all(f32[8,32,1024]{2,0,1:T(8,128)S(1)} %copy.108), channel_id=1, replica_groups=mesh['chan'=4,'pulse'=4,'range'=2] {'pulse'}, dimensions={1} | all-to-all | bytes 2097152 | tf_op jit(solution)/shard_map/all_to_all | solution.py:174
  360.5 0.6 copy.109
  361.2 2.4 collective-permute-start
  363.6 1.3 collective-permute-start.1
  364.9 0.3 collective-permute-done
  365.2 4.2 %collective-permute-done.1 = f32[8,8,20]{2,1,0:T(8,128)S(1)} collective-permute-done((f32[8,8,20]{2,1,0:T(8,128)S(1)}, f32[8,8,20]{2,1,0:T(8,128)S(1)}, u32[]{:S(2)}, u32[]{:S(2)}) %collective-permute-start.1) | collective-permute-done | bytes 5152 | tf_op jit(solution)/shard_map/ppermute | solution.py:21
  369.4 12.0 %fusion.14 = f32[8,8,4096]{2,1,0:T(8,128)} fusion(f32[8,8,4096]{2,1,0:T(8,128)S(1)} %bitcast.151, f32[8,8,20]{2,1,0:T(8,128)S(1)} %collective-permute-done.1, f32[8,8,20]{2,1,0:T(8,128)S(1)} %collective-permute-done), kind=kLoop, calls=%fused_computation.60 | loop fusion | flops 17301504 | bytes 2107392 | tf_op jit(solution)/shard_map/div | solution.py:193
  (23 shorter events, 0.9 us)
Async XLA Ops:
  10.6 6.5 %copy-start.2 = (bf16[2,32,64]{2,1,0:T(8,128)(2,1)S(1)}, bf16[2,32,64]{2,1,0:T(8,128)(2,1)}, u32[]{:S(2)}) copy-start(bf16[2,32,64]{2,1,0:T(8,128)(2,1)} %param.4) | copy-start | bytes 24580
  10.6 54.7 %all-to-all-start = ((bf16[2,16,8,4096]{3,1,0,2:T(8,128)(2,1)}), bf16[2,16,8,4096]{3,1,0,2:T(8,128)(2,1)S(1)}, u32[]{:S(2)}, u32[]{:S(2)}) async-start(bf16[2,16,8,4096]{3,1,0,2:T(8,128)(2,1)} %copy.81), calls=%async_computation | async-start | bytes 4194304 | tf_op jit(solution)/shard_map/all_to_all | solution.py:107
  17.1 115.6 %all-gather.4.cloned.1.call-start = ((), (), s32[]{:S(2)}) async-start(), calls=%async_computation.4 | async-start | bytes 3145728 | tf_op jit(solution)/shard_map/all_gather | solution.py:119
  99.3 1.3 copy-start.1
  100.4 112.5 %all-gather.6.cloned.1.call-start = ((), (), s32[]{:S(2)}) async-start(), calls=%async_computation.5 | async-start | bytes 3145728 | tf_op jit(solution)/shard_map/all_gather | solution.py:148
  176.5 1.5 copy-start
  179.7 67.9 %all-gather.8.cloned.1.call-start = ((), (), s32[]{:S(2)}) async-start(), calls=%async_computation.6 | async-start | bytes 3145728 | tf_op jit(solution)/shard_map/all_gather | solution.py:149
  361.2 4.0 %collective-permute-start = (f32[8,8,20]{2,1,0:T(8,128)S(1)}, f32[8,8,20]{2,1,0:T(8,128)S(1)}, u32[]{:S(2)}, u32[]{:S(2)}) collective-permute-start(f32[8,8,20]{2,1,0:T(8,128)S(1)} %get-tuple-element.13), channel_id=1, source_target_pairs={{0,1},{2,3},{4,5},{6,7},{8,9},{10,11},{12,13},{14,15},{16,17},{18,... | collective-permute-start | bytes 15368 | tf_op jit(solution)/shard_map/ppermute | solution.py:20
  363.6 5.8 %collective-permute-start.1 = (f32[8,8,20]{2,1,0:T(8,128)S(1)}, f32[8,8,20]{2,1,0:T(8,128)S(1)}, u32[]{:S(2)}, u32[]{:S(2)}) collective-permute-start(f32[8,8,20]{2,1,0:T(8,128)S(1)} %get-tuple-element.14), channel_id=1, source_target_pairs={{1,0},{3,2},{5,4},{7,6},{9,8},{11,10},{13,12},{15,14},{17,16},{19,... | collective-permute-start | bytes 15368 | tf_op jit(solution)/shard_map/ppermute | solution.py:21
Sparse Core Ops, SparseCore 0:
  100.5 32.1 all-gather.3
  179.8 33.0 all-gather.5
  214.5 33.0 all-gather.7
where the time goes:
time: 395 us; the launch traced here: 388 us
  waiting for transfers between devices  141 us (36%)
  local copies, waits for them, and re-layouts  112 us (28%)
  blocking collectives  61.8 us (16%)
  matrix products  24.9 us (6%)
  other arithmetic  24.3 us (6%)
  between operations  13.9 us (4%)
  starting transfers between devices  10.5 us (3%)
    unnamed x12, local copies, waits for them, and re-layouts  48.9 us
    all_to_all x1, waiting for transfers between devices, shards(): lax.all_to_all(signal, 'chan', split_axis=2, concat_axis=1, tiled=True)  48.2 us
    all_gather x1, waiting for transfers between devices, shards(): lax.all_gather(restored[1], 'range', axis=2, tiled=True)  34.7 us
    all_gather x1, waiting for transfers between devices, shards(): lax.all_gather(restored[0], 'range', axis=2, tiled=True)  32.5 us
    all_to_all x1, blocking collectives, shards(): lax.all_to_all(formed, 'chan', split_axis=1, concat_axis=2, tiled=True)  27.7 us
    all_gather x1, waiting for transfers between devices, shards(): shard_piece = lax.all_gather(beam_data, 'range', axis=3, tiled=True)  20.2 us
    all_to_all x1, blocking collectives, shards(): lax.all_to_all(compressed, 'pulse', split_axis=3, concat_axis=2, tiled=True)  17.2 us
    all_to_all x1, blocking collectives, shards(): lax.all_to_all(mixed_real * mixed_real + mixed_imag * mixed_imag, 'pulse'...  16.9 us
  transfers between devices with their start and end apart: 6, of which 6 were waited for; matrix products, arithmetic and copies ran while one was open for 3% of the time, Pallas kernels for 0%

commit v1 on v0

--- a/solution.py
+++ b/solution.py
@@ -1,3 +1,4 @@
+import functools
 import math
 import jax
 import jax.numpy as jnp
@@ -8,6 +9,39 @@
 TRAIN = 16
 PRECISE = lax.Precision.HIGHEST
 NOISE_FLOOR = 0.25
+
+
+def balance_routes_all(mat, at_axis, arr_in):
+    then, aux = (mat.shape[:at_axis], mat.shape[at_axis + 1 :])
+    block_out = jnp.moveaxis(mat.reshape(*then, arr_in, -1, *aux), at_axis, 0)
+    return block_out
+
+
+def define_levels_all_here(inner_x, join_dim):
+    big = list(inner_x.shape[1:])
+    big[join_dim] *= inner_x.shape[0]
+    mid_arr = jnp.moveaxis(inner_x, 0, join_dim).reshape(big)
+    return mid_arr
+
+
+def manage_the_region(page, device_axis, local_x, u_in):
+    right_arr, step_out = (lax.psum(1, axis_name=device_axis), lax.axis_index(device_axis))
+    state_now = balance_routes_all(page, local_x, right_arr)
+    t1 = state_now
+    u = 1
+    while u < right_arr:
+        met_up, s_next = ((step_out + u) % right_arr, (step_out - u) % right_arr)
+        later = lax.dynamic_index_in_dim(state_now, met_up, 0)
+        z = lax.ppermute(
+            later, device_axis, tuple(((jj, (jj + u) % right_arr) for jj in range(right_arr)))
+        )
+        t1 = lax.dynamic_update_slice_in_dim(t1, z, s_next, axis=0)
+        u += 1
+    part_now = define_levels_all_here(t1, u_in)
+    return part_now
+
+
+bind_tables = functools.partial(manage_the_region, device_axis="chan", local_x=1, u_in=2)
 
 
 def padded_2(x, sides, width):
@@ -110,7 +144,7 @@
     flat_samples = samples.reshape(2 * chan_count, pulses_here * gates_here)
     formed = jnp.dot(stacked, flat_samples, preferred_element_type=jnp.float32)
     formed = formed.astype(jnp.bfloat16).reshape(2, beam_count, pulses_here, gates_here)
-    beam_data = lax.all_to_all(formed, "chan", split_axis=1, concat_axis=2, tiled=True)
+    beam_data = bind_tables(formed)
     beam_local = beam_data.shape[1]
     range_count = lax.axis_size("range")
     range_index = lax.axis_index("range")

time: 395 us -> 396 us (level)
  blocking collectives: 61.8 us -> 34.1 us
  waiting for transfers between devices: 141 us -> 157 us
  other arithmetic: 24.3 us -> 30 us
  local copies, waits for them, and re-layouts: 112 us -> 116 us
    all_to_all x1 -> x0, blocking collectives: 27.7 us -> none  [shards(): lax.all_to_all(formed, 'chan', split_axis=1, concat_axis=2, tiled=True)]
    ppermute x0 -> x3, waiting for transfers between devices: none -> 19.9 us  [manage_the_region(): lax.ppermute(later, device_axis, tuple(((jj, (jj + u) % right_arr) for jj...]
    reshape x2 -> x3, local copies, waits for them, and re-layouts: 1.7 us -> 8.79 us  [the longest x1 4.03 us: shards(): shard_piece[1].reshape(beam_local, pulse_local, shard_count, gate_count)]
    reduce_sum x1, other arithmetic: 3.16 us -> 7.61 us  [shards(): sum_real = jnp.sum(rows_real * cos_part - rows_imag * sin_part, axis=2)]
    unnamed x12 -> x10, local copies, waits for them, and re-layouts: 48.9 us -> 47.7 us
  transfers between devices with their start and end apart: 6 -> 9, of which waited for: 6 -> 8; matrix products, arithmetic and copies ran while one was open for 3% -> 4% of each run, Pallas kernels for 0% -> 0%
where the time goes in v1:
time: 396 us; the launch traced here: 390 us
  waiting for transfers between devices  157 us (40%)
  local copies, waits for them, and re-layouts  116 us (29%)
  blocking collectives  34.1 us (9%)
  other arithmetic  30 us (8%)
  matrix products  24.3 us (6%)
  starting transfers between devices  14.3 us (4%)
  between operations  14 us (4%)
    all_to_all x1, waiting for transfers between devices, shards(): lax.all_to_all(signal, 'chan', split_axis=2, concat_axis=1, tiled=True)  48.2 us
    unnamed x10, local copies, waits for them, and re-layouts  47.7 us
    all_gather x1, waiting for transfers between devices, shards(): lax.all_gather(restored[0], 'range', axis=2, tiled=True)  32.5 us
    all_gather x1, waiting for transfers between devices, shards(): lax.all_gather(restored[1], 'range', axis=2, tiled=True)  31.4 us
    ppermute x3, waiting for transfers between devices, manage_the_region(): lax.ppermute(later, device_axis, tuple(((jj, (jj + u) % right_arr) for jj...  19.9 us
    all_gather x1, waiting for transfers between devices, shards(): shard_piece = lax.all_gather(beam_data, 'range', axis=3, tiled=True)  19.7 us
    all_to_all x1, blocking collectives, shards(): lax.all_to_all(compressed, 'pulse', split_axis=3, concat_axis=2, tiled=True)  17.2 us
    all_to_all x1, blocking collectives, shards(): lax.all_to_all(mixed_real * mixed_real + mixed_imag * mixed_imag, 'pulse'...  16.9 us
  transfers between devices with their start and end apart: 9, of which 8 were waited for; matrix products, arithmetic and copies ran while one was open for 4% of the time, Pallas kernels for 0%

profile of v1, /device:TPU:0, one launch (start us, length us, event | category | flops | bytes accessed | tf_op | source)
XLA Modules:
  0.0 389.7 jit_solution(9948941066630835210)
XLA Ops:
  6.5 4.1 %copy.35 = bf16[2,16,8,4096]{3,1,0,2:T(8,128)(2,1)} copy(bf16[2,16,8,4096]{3,2,1,0:T(8,128)(2,1)} %param.3) | data formatting | bytes 4194304 | tf_op args[0]
  10.6 6.5 %all-to-all-start = ((bf16[2,16,8,4096]{3,1,0,2:T(8,128)(2,1)}), bf16[2,16,8,4096]{3,1,0,2:T(8,128)(2,1)S(1)}, u32[]{:S(2)}, u32[]{:S(2)}) async-start(bf16[2,16,8,4096]{3,1,0,2:T(8,128)(2,1)} %copy.35), calls=%async_computation | async-start | bytes 4194304 | tf_op jit(solution)/shard_map/all_to_all | solution.py:141
  17.1 48.2 %all-to-all-done = bf16[2,16,8,4096]{3,1,0,2:T(8,128)(2,1)S(1)} async-done(((bf16[2,16,8,4096]{3,1,0,2:T(8,128)(2,1)}), bf16[2,16,8,4096]{3,1,0,2:T(8,128)(2,1)S(1)}, u32[]{:S(2)}, u32[]{:S(2)}) %all-to-all-start) | async-done | bytes 2097184 | tf_op jit(solution)/shard_map/all_to_all | solution.py:141
  65.3 2.2 copy.36
  67.5 1.3 copy.55
  68.8 0.5 convolution_convert_fusion
  69.5 3.7 collective-permute-start.2
  73.2 7.2 %collective-permute-done = bf16[1,2,8,2,4096]{4,2,3,0,1:T(8,128)(2,1)S(1)} collective-permute-done((bf16[1,2,8,2,4096]{4,2,3,0,1:T(8,128)(2,1)S(1)}, bf16[1,2,8,2,4096]{4,2,3,0,1:T(8,128)(2,1)S(1)}, u32[]{:S(2)}, u32[]{:S(2)}) %collective-permute-start) | collective-permute-done | bytes 262176 | tf_op jit(solution)/shard_map/ppermute | solution.py:35
  80.4 12.7 %collective-permute-done.1 = bf16[1,2,8,2,4096]{4,2,3,0,1:T(8,128)(2,1)S(1)} collective-permute-done((bf16[1,2,8,2,4096]{4,2,3,0,1:T(8,128)(2,1)S(1)}, bf16[1,2,8,2,4096]{4,2,3,0,1:T(8,128)(2,1)S(1)}, u32[]{:S(2)}, u32[]{:S(2)}) %collective-permute-start.1) | collective-permute-done | bytes 262176 | tf_op jit(solution)/shard_map/ppermute | solution.py:35
  93.2 1.5 copy.52
  94.8 0.3 all-gather.6.cloned.1.call-start
  95.1 6.4 %reshape.191 = f32[2,4096,2]{2,1,0:T(8,128)} reshape(f32[2,8192]{1,0:T(2,128)S(1)} %copy-done.1) | data formatting | bytes 131072 | tf_op jit(solution)/shard_map/reshape | solution.py:173
  101.5 4.8 %dynamic-slice_reduce_fusion = f32[2,4096]{1,0:T(2,128)S(1)} fusion(f32[2,4096,2]{2,1,0:T(8,128)} %reshape.191, s32[]{:T(128)S(6)} %select_n.191), kind=kLoop, calls=%fused_computation.31 | loop fusion | bytes 65540 | tf_op jit(solution)/shard_map/jit(dynamic_index_in_dim)/dynamic_slice | solution.py:174
  106.3 0.1 reshape.192
  106.8 0.1 sine_negate_fusion
  106.9 0.1 broadcast_multiply_fusion
  107.0 19.7 %all-gather.4.cloned.1.call-done = bf16[2,8,8,8192]{3,2,1,0:T(8,128)(2,1)} async-done(((bf16[2,8,8,4096]{3,2,1,0:T(8,128)(2,1)}), bf16[2,8,8,8192]{3,2,1,0:T(8,128)(2,1)}) %all-gather.4.cloned.1.call-update) | async-done | bytes 2097168 | tf_op jit(solution)/shard_map/all_gather | solution.py:153
  126.7 3.9 %fusion.275 = (f32[1,8,8,8192]{3,2,1,0:T(8,128)}, f32[1,8,8,8192]{3,2,1,0:T(8,128)}) fusion(bf16[2,8,8,8192]{3,2,1,0:T(8,128)(2,1)} %all-gather.4.cloned.1.call-done), kind=kLoop, calls=%fused_computation.370 | loop fusion | bytes 8388608 | tf_op jit(solution)/shard_map/slice | solution.py:164
  130.6 3.0 squeeze.26
  133.6 4.0 %squeeze.27 = f32[8,8,2,4096]{3,2,1,0:T(2,128)} reshape(f32[1,8,8,8192]{3,2,1,0:T(8,128)} %get-tuple-element.12) | data formatting | bytes 4194304 | tf_op jit(solution)/shard_map/squeeze | solution.py:164
  137.7 8.0 %subtract_reduce_fusion.1 = (f32[8,8,4096]{2,1,0:T(8,128)S(1)}, f32[8,8,4096]{2,1,0:T(8,128)S(1)}) fusion(f32[8,8,2,4096]{3,2,1,0:T(2,128)} %squeeze.27, f32[8,8,2,4096]{3,2,1,0:T(2,128)S(1)} %squeeze.26, f32[2]{0:T(128)S(1)} %get-tuple-element.23, f32[2]{0:T(128)S(1)} %get-tuple-element.22), kind=kLoop, calls=%fused_computation.35 | loop fusion | flops 3670016 | bytes 6291472 | tf_op jit(solution)/shard_map/reduce_sum | solution.py:164
  145.7 1.4 fusion.84
  147.1 1.4 fusion.88
  148.5 1.4 fusion.2
  150.0 1.4 fusion.3
  151.4 1.2 fusion.78
  152.6 1.2 fusion.79
  153.9 1.2 convolution_add_fusion.2
  155.1 1.2 convolution_subtract_fusion.2
  156.3 1.2 fusion.80
  157.6 1.4 fusion.81
  159.0 1.2 convolution_add_fusion.1
  160.2 1.2 convolution_subtract_fusion.1
  161.4 1.2 fusion.83
  162.6 1.2 fusion.82
  163.8 2.2 fusion
  166.0 2.4 reshape.194
  168.4 2.2 fusion.1
  170.5 1.5 reshape.193
  172.1 1.6 multiply_subtract_fusion
  173.8 0.7 all-gather.8.cloned.1.call-update
  174.5 32.5 %all-gather.6.cloned.1.call-done = f32[8,8,8192]{2,1,0:T(8,128)} async-done(((f32[8,8,4096]{2,1,0:T(8,128)}), f32[8,8,8192]{2,1,0:T(8,128)}) %all-gather.6.cloned.1.call-update) | async-done | bytes 2097168 | tf_op jit(solution)/shard_map/all_gather | solution.py:182
  207.0 3.2 reshape.195
  210.2 31.4 %all-gather.8.cloned.1.call-done = f32[8,8,8192]{2,1,0:T(8,128)} async-done(((f32[8,8,4096]{2,1,0:T(8,128)}), f32[8,8,8192]{2,1,0:T(8,128)}) %all-gather.8.cloned.1.call-update) | async-done | bytes 2097168 | tf_op jit(solution)/shard_map/all_gather | solution.py:183
  241.6 4.0 %reshape.196 = f32[8,8,2,4096]{3,2,1,0:T(2,128)} reshape(f32[8,8,8192]{2,1,0:T(8,128)} %all-gather.8.cloned.1.call-done) | data formatting | bytes 4194304 | tf_op jit(solution)/shard_map/reshape | solution.py:187
  245.7 7.6 %subtract_reduce_fusion = (f32[8,8,4096]{2,1,0:T(8,128)S(1)}, f32[8,8,4096]{2,1,0:T(8,128)S(1)}) fusion(f32[8,8,2,4096]{3,2,1,0:T(2,128)} %reshape.196, f32[8,8,2,4096]{3,2,1,0:T(2,128)S(1)} %reshape.195, f32[2]{0:T(128)S(1)} %fusion.202, f32[2]{0:T(128)S(1)} %get-tuple-element.22), kind=kLoop, calls=%fused_computation.33 | loop fusion | flops 3670016 | bytes 6291472 | tf_op jit(solution)/shard_map/reduce_sum | solution.py:194
  253.4 0.1 pad_maximum_fusion.2
  253.5 13.8 %copy.42 = bf16[2,8,8,4096]{2,1,0,3:T(8,128)(2,1)} copy(bf16[2,8,8,4096]{3,2,1,0:T(8,128)(2,1)S(1)} %pad_maximum_fusion.2) | data formatting | bytes 2097152 | tf_op jit(solution)/shard_map/stack | solution.py:196
  267.3 20.5 %reshape.206 = bf16[4,2,65536]{2,1,0:T(2,128)(2,1)S(1)} reshape(bf16[4096,2,8,8]{3,2,1,0:T(8,128)(2,1)} %bitcast.153) | data formatting | bytes 2097152
  287.9 17.2 %all_to_all.48 = bf16[4,2,65536]{2,1,0:T(2,128)(2,1)S(1)} all-to-all(bf16[4,2,65536]{2,1,0:T(2,128)(2,1)S(1)} %reshape.206), channel_id=1, replica_groups=mesh['chan'=4,'pulse'=4,'range'=2] {'pulse'}, dimensions={0} | all-to-all | bytes 2097152 | tf_op jit(solution)/shard_map/all_to_all | solution.py:201
  305.1 21.7 %reshape.207 = bf16[4096,2,8,8]{3,2,1,0:T(8,128)(2,1)} reshape(bf16[4,2,65536]{2,1,0:T(2,128)(2,1)S(1)} %all_to_all.48) | data formatting | bytes 2097152
  326.8 16.0 %copy.43 = bf16[2,8,8,4,1024]{4,2,3,1,0:T(8,128)(2,1)S(1)} copy(bf16[2,8,8,4,1024]{2,1,0,4,3:T(8,128)(2,1)} %bitcast.154) | data formatting | bytes 2097152 | tf_op jit(solution)/shard_map/all_to_all | solution.py:201
  342.8 0.4 fusion.76
  343.1 0.4 fusion.77
  343.5 0.4 fusion.7
  343.9 0.4 fusion.6
  344.2 0.6 copy.44
  344.9 16.9 %all_to_all.49 = f32[8,32,1024]{2,0,1:T(8,128)S(1)} all-to-all(f32[8,32,1024]{2,0,1:T(8,128)S(1)} %copy.44), channel_id=1, replica_groups=mesh['chan'=4,'pulse'=4,'range'=2] {'pulse'}, dimensions={1} | all-to-all | bytes 2097152 | tf_op jit(solution)/shard_map/all_to_all | solution.py:208
  361.7 0.6 copy.45
  362.4 2.4 collective-permute-start.3
  364.9 1.3 collective-permute-start.4
  366.2 0.3 collective-permute-done.3
  366.4 4.2 %collective-permute-done.4 = f32[8,8,20]{2,1,0:T(8,128)S(1)} collective-permute-done((f32[8,8,20]{2,1,0:T(8,128)S(1)}, f32[8,8,20]{2,1,0:T(8,128)S(1)}, u32[]{:S(2)}, u32[]{:S(2)}) %collective-permute-start.4) | collective-permute-done | bytes 5152 | tf_op jit(solution)/shard_map/ppermute | solution.py:55
  370.7 12.0 %fusion.14 = f32[8,8,4096]{2,1,0:T(8,128)} fusion(f32[8,8,4096]{2,1,0:T(8,128)S(1)} %bitcast.174, f32[8,8,20]{2,1,0:T(8,128)S(1)} %collective-permute-done.4, f32[8,8,20]{2,1,0:T(8,128)S(1)} %collective-permute-done.3), kind=kLoop, calls=%fused_computation.60 | loop fusion | flops 17301504 | bytes 2107392 | tf_op jit(solution)/shard_map/div | solution.py:227
  (29 shorter events, 0.9 us)
Async XLA Ops:
  10.6 6.5 %copy-start.2 = (bf16[2,32,64]{2,1,0:T(8,128)(2,1)S(1)}, bf16[2,32,64]{2,1,0:T(8,128)(2,1)}, u32[]{:S(2)}) copy-start(bf16[2,32,64]{2,1,0:T(8,128)(2,1)} %param.4) | copy-start | bytes 24580
  10.6 54.7 %all-to-all-start = ((bf16[2,16,8,4096]{3,1,0,2:T(8,128)(2,1)}), bf16[2,16,8,4096]{3,1,0,2:T(8,128)(2,1)S(1)}, u32[]{:S(2)}, u32[]{:S(2)}) async-start(bf16[2,16,8,4096]{3,1,0,2:T(8,128)(2,1)} %copy.35), calls=%async_computation | async-start | bytes 4194304 | tf_op jit(solution)/shard_map/all_to_all | solution.py:141
  17.1 109.6 %all-gather.4.cloned.1.call-start = ((), (), s32[]{:S(2)}) async-start(), calls=%async_computation.3 | async-start | bytes 3145728 | tf_op jit(solution)/shard_map/all_gather | solution.py:153
  69.3 11.0 %collective-permute-start = (bf16[1,2,8,2,4096]{4,2,3,0,1:T(8,128)(2,1)S(1)}, bf16[1,2,8,2,4096]{4,2,3,0,1:T(8,128)(2,1)S(1)}, u32[]{:S(2)}, u32[]{:S(2)}) collective-permute-start(bf16[1,2,8,2,4096]{4,2,3,0,1:T(8,128)(2,1)S(1)} %get-tuple-element.17), channel_id=1, source_target_pairs={{0,8},{8,16},{16,24},{24,0},{1,9},{9,17},{17,25},{25,1},{2,10},{10... | collective-permute-start | bytes 786440 | tf_op jit(solution)/shard_map/ppermute | solution.py:35
  69.5 23.7 %collective-permute-start.2 = (bf16[1,2,8,2,4096]{4,2,3,0,1:T(8,128)(2,1)S(1)}, bf16[1,2,8,2,4096]{4,2,3,0,1:T(8,128)(2,1)S(1)}, u32[]{:S(2)}, u32[]{:S(2)}) collective-permute-start(bf16[1,2,8,2,4096]{4,2,3,0,1:T(8,128)(2,1)S(1)} %get-tuple-element.15), channel_id=1, source_target_pairs={{0,24},{8,0},{16,8},{24,16},{1,25},{9,1},{17,9},{25,17},{2,26},{10... | collective-permute-start | bytes 786440 | tf_op jit(solution)/shard_map/ppermute | solution.py:35
  73.2 19.9 %collective-permute-start.1 = (bf16[1,2,8,2,4096]{4,2,3,0,1:T(8,128)(2,1)S(1)}, bf16[1,2,8,2,4096]{4,2,3,0,1:T(8,128)(2,1)S(1)}, u32[]{:S(2)}, u32[]{:S(2)}) collective-permute-start(bf16[1,2,8,2,4096]{4,2,3,0,1:T(8,128)(2,1)S(1)} %get-tuple-element.16), channel_id=1, source_target_pairs={{0,16},{8,24},{16,0},{24,8},{1,17},{9,25},{17,1},{25,9},{2,18},{10... | collective-permute-start | bytes 786440 | tf_op jit(solution)/shard_map/ppermute | solution.py:35
  80.4 14.7 %copy-start.1 = (f32[2,8192]{1,0:T(2,128)S(1)}, f32[2,8192]{1,0:T(2,128)}, u32[]{:S(2)}) copy-start(f32[2,8192]{1,0:T(2,128)} %param.5) | copy-start | bytes 196612
  94.8 112.2 %all-gather.6.cloned.1.call-start = ((), (), s32[]{:S(2)}) async-start(), calls=%async_computation.4 | async-start | bytes 3145728 | tf_op jit(solution)/shard_map/all_gather | solution.py:182
  170.5 1.5 copy-start
  173.7 67.9 %all-gather.8.cloned.1.call-start = ((), (), s32[]{:S(2)}) async-start(), calls=%async_computation.5 | async-start | bytes 3145728 | tf_op jit(solution)/shard_map/all_gather | solution.py:183
  362.4 4.0 %collective-permute-start.3 = (f32[8,8,20]{2,1,0:T(8,128)S(1)}, f32[8,8,20]{2,1,0:T(8,128)S(1)}, u32[]{:S(2)}, u32[]{:S(2)}) collective-permute-start(f32[8,8,20]{2,1,0:T(8,128)S(1)} %get-tuple-element.13), channel_id=1, source_target_pairs={{0,1},{2,3},{4,5},{6,7},{8,9},{10,11},{12,13},{14,15},{16,17},{18,... | collective-permute-start | bytes 15368 | tf_op jit(solution)/shard_map/ppermute | solution.py:54
  364.9 5.8 %collective-permute-start.4 = (f32[8,8,20]{2,1,0:T(8,128)S(1)}, f32[8,8,20]{2,1,0:T(8,128)S(1)}, u32[]{:S(2)}, u32[]{:S(2)}) collective-permute-start(f32[8,8,20]{2,1,0:T(8,128)S(1)} %get-tuple-element.14), channel_id=1, source_target_pairs={{1,0},{3,2},{5,4},{7,6},{9,8},{11,10},{13,12},{15,14},{17,16},{19,... | collective-permute-start | bytes 15368 | tf_op jit(solution)/shard_map/ppermute | solution.py:55
Sparse Core Ops, SparseCore 0:
  94.9 31.6 all-gather.3
  173.8 33.0 all-gather.5
  208.5 33.0 all-gather.7
